TPU v7x, 128 devices: a whole 4x4x4 slice. The times are simulated.
128 devices in a mesh: row: 8 (over x, y_hi), col: 16 (over z, y_lo, core).
Axes of the slice: x: 4, y: 4 (y_hi: 2, y_lo: 2; y = y_hi * 2 + y_lo), z: 4, core: 2. Of those that a mesh axis runs over, the one named last changes fastest.
Arguments:
- old_residual: float32 [8192, 16384], P(('row', 'col')), may hold values from -6 to 6
- group_map: int32 [128, 8], replicated, may hold values from 0 to 1023, as said below
- q_factor: float32 [16384, 32], P('col', 'row'), may hold values from -0.046875 to 0.046875
Outputs:
- relaid: float32 [8192, 16384], P('row', 'col')
- projection: float32 [32, 8192], P(None, ('row', 'col'))
- row_norms: float32 [8192], P(('row', 'col'))
Inputs may be any that keep to these rules, and one draw needn't show every extreme that they name: `group_map`: all entries together are each group id 0 to 1023 once; row d (old device d) holds exactly one id of each range k * 128 to (k + 1) * 128 - 1, in any slot order.
All inputs are finite; a program needn't handle non-finite values.
Results may differ from a plain program's by a relative error of at most 0.00007.
Values sent between devices are 32-bit elements; how exact they have to be, the bound alone decides.
No kernel may reach another device: no remote copies, remote signals or barrier semaphores. Data moves between devices by JAX's collectives and lax.ppermute only.
A program may use at most 64 MiB of HBM per device.

v0:
```python
import jax
import jax.numpy as jnp
from jax import lax
from jax.sharding import PartitionSpec as P

epsilon = 1e-06


def sent_to_all(shard, axis):
    count = lax.axis_size(axis)
    return lax.all_to_all(
        jnp.broadcast_to(shard[None], (count, *shard.shape)), axis, 0, 0, tiled=True
    )


def laid_out(tiles, dim):
    tiles = jnp.moveaxis(tiles, 0, dim)
    shape = tiles.shape
    return tiles.reshape(*shape[:dim], shape[dim] * shape[dim + 1], *shape[dim + 2 :])


def gathered_copies(shard, axis, dim):
    tiles = sent_to_all(shard, axis)
    return laid_out(tiles, dim)


def cut_along(shard, dim, count):
    before, after = (shard.shape[:dim], shard.shape[dim + 1 :])
    return jnp.moveaxis(shard.reshape(*before, count, -1, *after), dim, 0)


def sum_at_owner(shard, axis, dim):
    count = lax.axis_size(axis)
    tiles = lax.all_to_all(cut_along(shard, dim, count), axis, 0, 0, tiled=True)
    return jnp.sum(tiles, axis=0)


def on_device(old_residual, group_map, q_factor):
    row_count = lax.axis_size("row")
    column_count = lax.axis_size("col")
    devices_all = row_count * column_count
    my_row = lax.axis_index("row")
    my_column = lax.axis_index("col")
    position = my_row * column_count + my_column
    group_rows = old_residual.shape[0] // row_count
    full_width = old_residual.shape[1]
    block_width = full_width // column_count
    own_ids = lax.dynamic_index_in_dim(group_map, position, 0, keepdims=False)
    sending = jnp.argsort(own_ids)
    stored = jnp.take(old_residual.reshape(row_count, group_rows, full_width), sending, axis=0)
    pieces = stored.reshape(row_count, group_rows, column_count, block_width).transpose(0, 2, 1, 3)
    flat_pieces = pieces.reshape(devices_all, group_rows, block_width)
    received = lax.all_to_all(flat_pieces, ("row", "col"), split_axis=0, concat_axis=0, tiled=True)
    sorted_map = jnp.sort(group_map, axis=1)
    arriving_ids = lax.dynamic_index_in_dim(sorted_map, my_row, 1, keepdims=False)
    placement = jnp.argsort(arriving_ids)
    arranged = jnp.take(received, placement, axis=0)
    relaid_block = arranged.reshape(devices_all * group_rows, block_width)
    factor_full = gathered_copies(q_factor, "row", 1)
    projected_share = sum_at_owner(
        jnp.dot(
            relaid_block,
            factor_full,
            precision=lax.Precision.HIGHEST,
            preferred_element_type=jnp.float32,
        ),
        "col",
        0,
    )
    squares = jnp.sum(relaid_block * relaid_block, axis=1)
    square_total = sum_at_owner(squares, "col", 0)
    row_norms = jnp.sqrt(square_total / full_width + epsilon)
    return (relaid_block, projected_share.T, row_norms)


def solution(mesh):
    placed = (P(("row", "col"), None), P(), P("col", "row"))
    return jax.shard_map(
        on_device,
        mesh=mesh,
        in_specs=placed,
        out_specs=(P("row", "col"), P(None, ("row", "col")), P(("row", "col"))),
        check_vma=False,
    )
```

profile of v0, /device:TPU:1, one launch (start us, length us, event | category | flops | bytes accessed | tf_op | source)
XLA Modules:
  0.0 125.2 jit_solution(10341393157861966837)
XLA Ops:
  0.6 1.4 %broadcast_in_dim.59 = f32[8,1024,4]{1,2,0:T(4,128)} broadcast(f32[1024,4]{0,1:T(4,128)} %param.5), dimensions={1,2} | broadcast | bytes 147456 | tf_op jit(solution)/shard_map/broadcast_in_dim | solution.py:12
  2.0 7.5 %all-to-all-start.1 = ((f32[8,1024,4]{1,2,0:T(4,128)}), f32[8,1024,4]{1,2,0:T(4,128)S(1)}, u32[]{:S(2)}, u32[]{:S(2)}) async-start(f32[8,1024,4]{1,2,0:T(4,128)} %broadcast_in_dim.59), calls=%async_computation.1 | async-start | bytes 262144 | tf_op jit(solution)/shard_map/all_to_all | solution.py:11
  9.5 0.9 dynamic-slice_reduce_fusion
  10.3 1.0 sort.51
  11.3 5.0 %gather_fusion = f32[8,8,16384]{2,1,0:T(8,128)} fusion(f32[8,8,16384]{2,1,0:T(8,128)} %bitcast.26, s32[1024]{0:T(1024)S(1)} %pad_clamp_fusion.1), kind=kCustom, calls=%fused_computation | custom fusion | bytes 8388640 | tf_op jit(solution)/shard_map/jit(_take)/gather | solution.py:50
  16.4 5.1 %broadcast_select_fusion.1 = f32[8,8,16,1024]{3,1,2,0:T(8,128)} fusion(f32[8,8,16,1024]{3,1,2,0:T(8,128)} %bitcast.25, pred[8]{0:T(512)(128)(4,1)S(1)} %compare_and_fusion), kind=kLoop, calls=%fused_computation.5 | loop fusion | flops 1048576 | bytes 8388616 | tf_op jit(solution)/shard_map/jit(_take)/select_n | solution.py:50
  21.5 0.0 all-to-all-done.1
  21.5 0.0 copy-start.1
  21.5 11.7 %all-to-all-start = ((f32[128,8,1024]{2,1,0:T(8,128)}), f32[128,8,1024]{2,1,0:T(8,128)}, u32[]{:S(2)}, u32[]{:S(2)}) async-start(f32[128,8,1024]{2,1,0:T(8,128)} %bitcast.23), calls=%async_computation | async-start | bytes 8388608 | tf_op jit(solution)/shard_map/all_to_all | solution.py:53
  33.2 0.0 copy-done.1
  33.2 0.7 sort.49
  33.8 2.5 %sort.50 = (s32[128]{0:T(128)}, s32[128]{0:T(128)S(1)}) sort(s32[128]{0:T(128)S(1)} %dynamic-slice_bitcast_fusion, s32[128]{0:T(128)S(1)} %iota.12), dimensions={0}, to_apply=%region_1.2 | sort | flops 896 | bytes 2048 | tf_op jit(solution)/shard_map/jit(argsort)/sort | solution.py:56
  36.4 0.1 broadcast_in_dim.54
  36.5 0.1 broadcast_in_dim.46
  36.6 0.1 broadcast_in_dim.47
  36.7 0.1 broadcast_bitcast_fusion
  36.8 49.1 %all-to-all-done = f32[128,8,1024]{2,1,0:T(8,128)} async-done(((f32[128,8,1024]{2,1,0:T(8,128)}), f32[128,8,1024]{2,1,0:T(8,128)}, u32[]{:S(2)}, u32[]{:S(2)}) %all-to-all-start) | async-done | bytes 4194336 | tf_op jit(solution)/shard_map/all_to_all | solution.py:53
  85.9 5.0 %gather_fusion.1 = f32[128,8,1024]{2,1,0:T(8,128)} fusion(f32[128,8,1024]{2,1,0:T(8,128)} %all-to-all-done, s32[1024]{0:T(1024)S(1)} %pad_clamp_fusion), kind=kCustom, calls=%fused_computation.1 | custom fusion | bytes 8389120 | tf_op jit(solution)/shard_map/jit(_take)/gather | solution.py:57
  90.9 0.0 copy-start
  90.9 4.7 %bitcast_select_fusion = f32[1024,1024]{1,0:T(8,128)} fusion(f32[128,8,1024]{2,1,0:T(8,128)} %gather_fusion.1, pred[1024]{0:T(1024)(128)(4,1)S(1)} %broadcast_in_dim.47), kind=kLoop, calls=%fused_computation.2 | loop fusion | flops 1048576 | bytes 8389632 | tf_op jit(solution)/shard_map/jit(_take)/select_n | solution.py:57
  95.6 0.0 copy-done
  95.6 2.4 %multiply_reduce_fusion = (f32[128,8]{1,0:T(8,128)S(1)}, f32[128,8,1024]{2,1,0:T(8,128)}) fusion(f32[128,8,1024]{2,1,0:T(8,128)S(1)} %copy-done, pred[128]{0:T(512)(128)(4,1)S(1)} %compare_and_fusion.1, pred[128,8]{1,0:T(8,128)(4,1)S(1)} %broadcast_bitcast_fusion), kind=kLoop, calls=%fused_computation.3 | loop fusion | flops 4193280 | bytes 8393856 | tf_op jit(solution)/shard_map/reduce_sum | solution.py:70
  98.1 0.7 all_to_all.18
  98.7 4.2 %all-to-all-start.3 = ((f32[16,1,64]{2,1,0:T(1,128)}), f32[16,1,64]{2,1,0:T(1,128)S(1)}, u32[]{:S(2)}, u32[]{:S(2)}) async-start(f32[16,1,64]{2,1,0:T(1,128)} %bitcast.10), calls=%async_computation.3 | async-start | bytes 16384 | tf_op jit(solution)/shard_map/all_to_all | solution.py:34
  102.9 7.4 %convolution_bitcast_fusion = f32[16,32,64]{2,1,0:T(8,128)S(1)} fusion(f32[16,64,1024]{2,1,0:T(8,128)} %bitcast.24, f32[1024,32,1]{0,1,2:T(8,128)S(1)} %reshape.103), kind=kOutput, calls=%fused_computation.16 | convolution fusion | flops 402653184 | bytes 4456448 | tf_op jit(solution)/shard_map/dot_general | solution.py:61
  110.3 0.8 reshape.106
  111.1 0.0 all-to-all-done.3
  111.1 5.8 %all-to-all-start.2 = ((f32[16,1,2048]{2,1,0:T(1,128)}), f32[16,1,2048]{2,1,0:T(1,128)S(1)}, u32[]{:S(2)}, u32[]{:S(2)}) async-start(f32[16,1,2048]{2,1,0:T(1,128)} %reshape.106), calls=%async_computation.2 | async-start | bytes 262144 | tf_op jit(solution)/shard_map/all_to_all | solution.py:34
  117.0 0.5 add_sqrt_fusion
  117.5 5.6 %all-to-all-done.2 = f32[16,1,2048]{2,1,0:T(1,128)S(1)} async-done(((f32[16,1,2048]{2,1,0:T(1,128)}), f32[16,1,2048]{2,1,0:T(1,128)S(1)}, u32[]{:S(2)}, u32[]{:S(2)}) %all-to-all-start.2) | async-done | bytes 131104 | tf_op jit(solution)/shard_map/all_to_all | solution.py:34
  123.0 0.5 broadcast.61
  123.5 0.9 reduce.4
  124.5 0.1 reshape.107
  124.6 0.6 bitcast_reduce_fusion
  (12 shorter events, 0.1 us)
Async XLA Ops:
  2.0 19.5 %all-to-all-start.1 = ((f32[8,1024,4]{1,2,0:T(4,128)}), f32[8,1024,4]{1,2,0:T(4,128)S(1)}, u32[]{:S(2)}, u32[]{:S(2)}) async-start(f32[8,1024,4]{1,2,0:T(4,128)} %broadcast_in_dim.59), calls=%async_computation.1 | async-start | bytes 262144 | tf_op jit(solution)/shard_map/all_to_all | solution.py:11
  21.5 11.7 %copy-start.1 = (s32[128,8]{0,1:T(8,128)S(1)}, s32[128,8]{0,1:T(8,128)}, u32[]{:S(2)}) copy-start(s32[128,8]{0,1:T(8,128)} %param.4) | copy-start | bytes 12292
  21.5 64.5 %all-to-all-start = ((f32[128,8,1024]{2,1,0:T(8,128)}), f32[128,8,1024]{2,1,0:T(8,128)}, u32[]{:S(2)}, u32[]{:S(2)}) async-start(f32[128,8,1024]{2,1,0:T(8,128)} %bitcast.23), calls=%async_computation | async-start | bytes 8388608 | tf_op jit(solution)/shard_map/all_to_all | solution.py:53
  90.9 4.7 %copy-start = (f32[128,8,1024]{2,1,0:T(8,128)S(1)}, f32[128,8,1024]{2,1,0:T(8,128)}, u32[]{:S(2)}) copy-start(f32[128,8,1024]{2,1,0:T(8,128)} %gather_fusion.1) | copy-start | bytes 12582916
  98.7 12.4 %all-to-all-start.3 = ((f32[16,1,64]{2,1,0:T(1,128)}), f32[16,1,64]{2,1,0:T(1,128)S(1)}, u32[]{:S(2)}, u32[]{:S(2)}) async-start(f32[16,1,64]{2,1,0:T(1,128)} %bitcast.10), calls=%async_computation.3 | async-start | bytes 16384 | tf_op jit(solution)/shard_map/all_to_all | solution.py:34
  111.1 11.9 %all-to-all-start.2 = ((f32[16,1,2048]{2,1,0:T(1,128)}), f32[16,1,2048]{2,1,0:T(1,128)S(1)}, u32[]{:S(2)}, u32[]{:S(2)}) async-start(f32[16,1,2048]{2,1,0:T(1,128)} %reshape.106), calls=%async_computation.2 | async-start | bytes 262144 | tf_op jit(solution)/shard_map/all_to_all | solution.py:34
where the time goes:
time: 126 us; the launch traced here: 125 us
  waiting for transfers between devices  54.6 us (43%)
  starting transfers between devices  29.1 us (23%)
  other arithmetic  18.6 us (15%)
  local copies, waits for them, and re-layouts  14.8 us (12%)
  matrix products  7.39 us (6%)
    all_to_all x1, waiting for transfers between devices, on_device(): lax.all_to_all(flat_pieces, ('row', 'col'), split_axis=0, concat_axis=0,...  49.1 us
    all_to_all x1, starting transfers between devices, on_device(): lax.all_to_all(flat_pieces, ('row', 'col'), split_axis=0, concat_axis=0,...  11.7 us
    all_to_all x2, starting transfers between devices, sum_at_owner(): tiles = lax.all_to_all(cut_along(shard, dim, count), axis, 0, 0, tiled=True)  9.96 us
    all_to_all x1, starting transfers between devices, sent_to_all(): lax.all_to_all(jnp.broadcast_to(shard[None], (count, *shard.shape)), axis...  7.47 us
    dot_general x1, matrix products, on_device(): jnp.dot(relaid_block, factor_full, precision=lax.Precision.HIGHEST, prefe...  7.39 us
    all_to_all x2, waiting for transfers between devices, sum_at_owner(): tiles = lax.all_to_all(cut_along(shard, dim, count), axis, 0, 0, tiled=True)  5.55 us
    select_n x2, other arithmetic, on_device(): jnp.take(old_residual.reshape(row_count, group_rows, full_width), sending...  5.11 us
    gather x1, local copies, waits for them, and re-layouts, on_device(): jnp.take(old_residual.reshape(row_count, group_rows, full_width), sending...  5.02 us
  transfers between devices with their start and end apart: 4, of which 2 were waited for; matrix products, arithmetic and copies ran while one was open for 19% of the time, Pallas kernels for 0%

commit v1 on v0

v1 whole, which is shorter than its diff:
```python
import jax
import jax.numpy as jnp
from jax import lax
from jax.experimental import pallas as pl
from jax.experimental.pallas import tpu as pltpu
from jax.sharding import Mesh, PartitionSpec as P

epsilon = 1e-06
ROW = ("x", "yh")
COL = ("z", "yl", "core")
ALL = ROW + COL


def order_slots(ids_ref, where_ref, source_ref, out_ref, sems):
    count = source_ref.shape[0]
    copies = []
    for slot in range(count):
        block = ids_ref[slot, where_ref[0]] // where_ref[1]
        copy = pltpu.make_async_copy(source_ref.at[slot], out_ref.at[block], sems.at[slot])
        copy.start()
        copies.append(copy)
    for copy in copies:
        copy.wait()


def place_and_reduce(place_ref, factor_ref, received_ref, relaid_ref, share_ref, data, sums, load_sems, store_sem):
    blocks, per_block, rows, width = data.shape
    rank = factor_ref.shape[0]
    loads = [
        pltpu.make_async_copy(received_ref.at[pl.ds(b * per_block, per_block)], data.at[b], load_sems.at[b])
        for b in range(blocks)
    ]
    for load in loads:
        load.start()
    factor = factor_ref[...]
    factor_high = factor.astype(jnp.bfloat16)
    factor_low = (factor - factor_high.astype(jnp.float32)).astype(jnp.bfloat16)
    filler = jnp.zeros((128 - 2 * rank, width), jnp.bfloat16)
    factors = jnp.concatenate([factor_high, factor_low, filler], axis=0)
    lane = lax.broadcasted_iota(jnp.int32, (per_block * rows, 128), 1)
    for b in range(blocks):
        loads[b].wait()
        for i in range(per_block):
            place = place_ref[b * per_block + i]
            pltpu.make_async_copy(data.at[b, i], relaid_ref.at[place], store_sem).start()
        part = data[b].reshape(per_block * rows, width)
        high = part.astype(jnp.bfloat16)
        low = (part - high.astype(jnp.float32)).astype(jnp.bfloat16)
        over = (((1,), (1,)), ((), ()))
        product = lax.dot_general(high, factors, over, preferred_element_type=jnp.float32)
        product += lax.dot_general(low, factors, over, preferred_element_type=jnp.float32)
        squares = jnp.sum(part * part, axis=1, keepdims=True)
        product = jnp.where(lane == 2 * rank, squares, product)
        for i in range(per_block):
            place = place_ref[b * per_block + i]
            sums[pl.ds(pl.multiple_of(place * rows, rows), rows), :] = product[i * rows : (i + 1) * rows]
    half = rank // 2
    for c in range(0, share_ref.shape[0], 2):
        turned = sums[c * 64 : (c + 2) * 64, :].T
        shares = turned[:rank] + turned[rank : 2 * rank]
        squares = turned[2 * rank : 2 * rank + 8]
        for i in range(2):
            lanes = slice(i * 64, (i + 1) * 64)
            share_ref[c + i, :half, :] = jnp.concatenate([shares[:half, lanes], shares[half:, lanes]], axis=1)
            share_ref[c + i, half:, :] = jnp.concatenate([squares[:, lanes], squares[:, lanes]], axis=1)
    pltpu.make_async_copy(data, data, store_sem).wait()


def finish(shares_ref, projection_ref, norms_ref, *, full_width):
    half = projection_ref.shape[0] // 2
    total = jnp.sum(shares_ref[...], axis=0)
    projection_ref[:half, :] = total[:half, :64]
    projection_ref[half:, :] = total[:half, 64:]
    norms_ref[...] = jnp.sqrt(total[half : half + 1, :64] / full_width + epsilon)


def gathered_factor(shard):
    other = lax.ppermute(shard, "yh", [(0, 1), (1, 0)])
    low = lax.axis_index("yh") == 0
    pair = jnp.stack([jnp.where(low, shard, other), jnp.where(low, other, shard)])
    count = lax.axis_size("x")
    tiles = [pair]
    for step in range(1, count):
        tiles.append(lax.ppermute(pair, "x", [(i, (i - step) % count) for i in range(count)]))
    ring = jnp.roll(jnp.stack(tiles), lax.axis_index("x"), axis=0)
    return ring.reshape(-1, shard.shape[1])


def on_device(old_residual, group_map, q_factor):
    rows_total = lax.axis_size(ROW)
    columns_total = lax.axis_size(COL)
    devices = rows_total * columns_total
    my_row = lax.axis_index(ROW)
    position = lax.axis_index(ALL)
    group_rows = old_residual.shape[0] // rows_total
    full_width = old_residual.shape[1]
    width = full_width // columns_total
    rank = q_factor.shape[1] * rows_total
    own_rows = devices * group_rows // columns_total
    ids = group_map.T.astype(jnp.int32)
    source = old_residual.reshape(rows_total, group_rows, columns_total, width).transpose(0, 2, 1, 3)
    any_space = pl.BlockSpec(memory_space=pl.ANY)
    smem = pl.BlockSpec(memory_space=pltpu.SMEM)
    vmem = pl.BlockSpec(memory_space=pltpu.VMEM)
    pieces = pl.pallas_call(
        order_slots,
        out_shape=jax.ShapeDtypeStruct(source.shape, jnp.float32),
        in_specs=[smem, smem, any_space],
        out_specs=any_space,
        scratch_shapes=[pltpu.SemaphoreType.DMA((rows_total,))],
        name="order_slots",
    )(ids, jnp.stack([position, jnp.int32(devices)]), source)
    pieces = pieces.reshape(devices, group_rows, width)
    received = lax.all_to_all(pieces, ALL, 0, 0, tiled=True)
    factor = gathered_factor(q_factor.T)
    place = jnp.sum(jnp.where(ids // devices == my_row, ids % devices, 0), axis=0)
    blocks = 8
    relaid, shares = pl.pallas_call(
        place_and_reduce,
        out_shape=(
            jax.ShapeDtypeStruct((devices, group_rows, width), jnp.float32),
            jax.ShapeDtypeStruct((columns_total, rank // 2 + 8, 2 * own_rows), jnp.float32),
        ),
        in_specs=[smem, vmem, any_space],
        out_specs=(any_space, vmem),
        scratch_shapes=[
            pltpu.VMEM((blocks, devices // blocks, group_rows, width), jnp.float32),
            pltpu.VMEM((devices * group_rows, 128), jnp.float32),
            pltpu.SemaphoreType.DMA((blocks,)),
            pltpu.SemaphoreType.DMA,
        ],
        name="place_and_reduce",
    )(place, factor, received)
    shares = lax.all_to_all(shares, COL, 0, 0, tiled=True)
    projection, norms = pl.pallas_call(
        lambda *refs: finish(*refs, full_width=full_width),
        out_shape=(
            jax.ShapeDtypeStruct((rank, own_rows), jnp.float32),
            jax.ShapeDtypeStruct((1, own_rows), jnp.float32),
        ),
        in_specs=[vmem],
        out_specs=(vmem, vmem),
        name="finish",
    )(shares)
    return relaid.reshape(devices * group_rows, width), projection, norms.reshape(own_rows)


def solution(mesh):
    parts = Mesh(mesh.devices.reshape(4, 2, 4, 2, 2), ALL)
    return jax.shard_map(
        on_device,
        mesh=parts,
        in_specs=(P(ALL, None), P(), P(COL, ROW)),
        out_specs=(P(ROW, COL), P(None, ALL), P(ALL)),
        check_vma=False,
    )
```

time: 126 us -> 222 us (1.76)
  Pallas kernels: 0 us -> 137 us
  blocking collectives: 0 us -> 18.3 us
  other arithmetic: 18.6 us -> 1.16 us
  waiting for transfers between devices: 54.6 us -> 37.4 us
  local copies, waits for them, and re-layouts: 14.8 us -> 0.8 us
  matrix products: 7.39 us -> 0 us
  starting transfers between devices: 29.1 us -> 26.1 us
    pallas_call x0 -> x3, Pallas kernels: none -> 137 us  [the longest x1 129 us: on_device(): pl.pallas_call(order_slots, out_shape=jax.ShapeDtypeStruct(source.shape,...]
    all_to_all x4 -> x1, waiting for transfers between devices: 54.6 us -> 0.4 us  [on_device(): received = lax.all_to_all(pieces, ALL, 0, 0, tiled=True)]
    ppermute x0 -> x4, waiting for transfers between devices: none -> 37 us  [the longest x1 34.1 us: gathered_factor(): other = lax.ppermute(shard, 'yh', [(0, 1), (1, 0)])]
    all_to_all x0 -> x1, blocking collectives: none -> 18.3 us  [on_device(): shares = lax.all_to_all(shares, COL, 0, 0, tiled=True)]
    all_to_all x4 -> x1, starting transfers between devices: 29.1 us -> 12 us  [on_device(): received = lax.all_to_all(pieces, ALL, 0, 0, tiled=True)]
    ppermute x0 -> x4, starting transfers between devices: none -> 14.2 us  [the longest x3 11.2 us: gathered_factor(): lax.ppermute(pair, 'x', [(i, (i - step) % count) for i in range(count)])]
    gather x2 -> x0, local copies, waits for them, and re-layouts: 9.99 us -> none  [the longest x1 5.02 us: on_device(): jnp.take(old_residual.reshape(row_count, group_rows, full_width), sending...]
    select_n x4 -> x0, other arithmetic: 9.82 us -> none  [the longest x2 5.11 us: on_device(): jnp.take(old_residual.reshape(row_count, group_rows, full_width), sending...]
  transfers between devices with their start and end apart: 4 -> 5, of which waited for: 2 -> 4; matrix products, arithmetic and copies ran while one was open for 19% -> 1% of each run, Pallas kernels for 0% -> 0%
where the time goes in v1:
time: 222 us
  Pallas kernels  137 us (62%)
  waiting for transfers between devices  37.4 us (17%)
  starting transfers between devices  26.1 us (12%)
  blocking collectives  18.3 us (8%)
    pallas_call x1, Pallas kernels, on_device(): pl.pallas_call(order_slots, out_shape=jax.ShapeDtypeStruct(source.shape,...  129 us
    ppermute x1, waiting for transfers between devices, gathered_factor(): other = lax.ppermute(shard, 'yh', [(0, 1), (1, 0)])  34.1 us
    all_to_all x1, blocking collectives, on_device(): shares = lax.all_to_all(shares, COL, 0, 0, tiled=True)  18.3 us
    all_to_all x1, starting transfers between devices, on_device(): received = lax.all_to_all(pieces, ALL, 0, 0, tiled=True)  12 us
    ppermute x3, starting transfers between devices, gathered_factor(): lax.ppermute(pair, 'x', [(i, (i - step) % count) for i in range(count)])  11.2 us
    pallas_call x1, Pallas kernels, on_device(): pl.pallas_call(place_and_reduce, out_shape=(jax.ShapeDtypeStruct((devices...  6.84 us
  transfers between devices with their start and end apart: 5, of which 4 were waited for; matrix products, arithmetic and copies ran while one was open for 1% of the time, Pallas kernels for 0%

profile of v1, /device:TPU:1, one launch (start us, length us, event | category | flops | bytes accessed | tf_op | source)
XLA Modules:
  0.0 221.9 jit_solution(18346640310507466)
XLA Ops:
  0.6 0.6 pad_add_fusion.where_ref
  1.2 129.0 %order_slots.1 = f32[8,16,8,1024]{3,2,1,0:T(8,128)} custom-call(s32[8,128]{1,0:T(8,128)} %bitcast.30, s32[2]{0:T(128)} %pad_add_fusion.where_ref, f32[8,16,8,1024]{3,2,1,0:T(8,128)} %bitcast.29), custom_call_target="tpu_custom_call" | custom-call | tf_op jit(solution)/shard_map/order_slots/pallas_call | solution.py:105
  130.2 0.0 copy-start.1
  130.2 0.0 copy-start
  130.2 12.0 %all-to-all-start = ((f32[128,8,1024]{2,1,0:T(8,128)}), f32[128,8,1024]{2,1,0:T(8,128)}, u32[]{:S(2)}, u32[]{:S(2)}) async-start(f32[128,8,1024]{2,1,0:T(8,128)} %bitcast.28), calls=%async_computation | async-start | bytes 8388608 | tf_op jit(solution)/shard_map/all_to_all | solution.py:114
  142.2 0.0 copy-done.1
  142.2 2.9 %collective-permute-start = (f32[4,1024]{1,0:T(4,128)S(1)}, f32[4,1024]{1,0:T(4,128)S(1)}, u32[]{:S(2)}, u32[]{:S(2)}) collective-permute-start(f32[4,1024]{1,0:T(4,128)S(1)} %bitcast.31), channel_id=1, source_target_pairs={{0,16},{16,0},{1,17},{17,1},{2,18},{18,2},{3,19},{19,3},{4,20},{20... | collective-permute-start | bytes 49160 | tf_op jit(solution)/shard_map/ppermute | solution.py:78
  145.1 0.0 copy-done
  145.2 0.5 fusion.2.place_ref
  145.7 34.1 %collective-permute-done = f32[4,1024]{1,0:T(4,128)S(1)} collective-permute-done((f32[4,1024]{1,0:T(4,128)S(1)}, f32[4,1024]{1,0:T(4,128)S(1)}, u32[]{:S(2)}, u32[]{:S(2)}) %collective-permute-start) | collective-permute-done | bytes 16416 | tf_op jit(solution)/shard_map/ppermute | solution.py:78
  179.9 9.8 %collective-permute-start.2 = (f32[2,4,1024]{2,1,0:T(4,128)S(1)}, f32[2,4,1024]{2,1,0:T(4,128)S(1)}, u32[]{:S(2)}, u32[]{:S(2)}) collective-permute-start(f32[2,4,1024]{2,1,0:T(4,128)S(1)} %pad_maximum_fusion), channel_id=1, source_target_pairs={{0,64},{32,96},{64,0},{96,32},{1,65},{33,97},{65,1},{97,33},{2,66}... | collective-permute-start | bytes 98312 | tf_op jit(solution)/shard_map/ppermute | solution.py:84
  189.6 0.0 collective-permute-start.1
  189.6 1.5 collective-permute-start.3
  191.1 1.7 collective-permute-done.1
  192.8 0.0 collective-permute-done.2
  192.8 1.2 collective-permute-done.3
  194.1 0.7 reshape.21.factor_ref
  194.8 0.4 all-to-all-done.received_ref
  195.2 6.8 %place_and_reduce.1 = (f32[128,8,1024]{2,1,0:T(8,128)}, f32[16,24,128]{2,1,0:T(8,128)}) custom-call(s32[128]{0:T(128)} %fusion.2.place_ref, f32[32,1024]{1,0:T(8,128)} %reshape.21.factor_ref, f32[128,8,1024]{2,1,0:T(8,128)} %all-to-all-done.received_ref), custom_call_target="tpu_custom_call" | custom-call | tf_op jit(solution)/shard_map/place_and_reduce/pallas_call | solution.py:118
  202.1 18.3 %all_to_all.10.refs_0_ = f32[16,24,128]{2,1,0:T(8,128)} all-to-all(f32[16,24,128]{2,1,0:T(8,128)} %get-tuple-element.8), channel_id=1, replica_groups=mesh['x'=4,'yh'=2,'z'=4,'yl'=2,'core'=2] {'z','yl','core'}, dimensions={0} | all-to-all | bytes 393216 | tf_op jit(solution)/shard_map/all_to_all | solution.py:134
  220.3 1.6 finish.1
  (11 shorter events, 0.1 us)
Async XLA Ops:
  130.2 12.0 %copy-start.1 = (f32[1024,4]{0,1:T(4,128)S(1)}, f32[1024,4]{0,1:T(4,128)}, u32[]{:S(2)}) copy-start(f32[1024,4]{0,1:T(4,128)} %param.5) | copy-start | bytes 49156
  130.2 14.9 %copy-start = (s32[128,8]{0,1:T(8,128)S(1)}, s32[128,8]{0,1:T(8,128)}, u32[]{:S(2)}) copy-start(s32[128,8]{0,1:T(8,128)} %param.4) | copy-start | bytes 12292
  130.2 65.0 %all-to-all-start = ((f32[128,8,1024]{2,1,0:T(8,128)}), f32[128,8,1024]{2,1,0:T(8,128)}, u32[]{:S(2)}, u32[]{:S(2)}) async-start(f32[128,8,1024]{2,1,0:T(8,128)} %bitcast.28), calls=%async_computation | async-start | bytes 8388608 | tf_op jit(solution)/shard_map/all_to_all | solution.py:114
  142.2 37.6 %collective-permute-start = (f32[4,1024]{1,0:T(4,128)S(1)}, f32[4,1024]{1,0:T(4,128)S(1)}, u32[]{:S(2)}, u32[]{:S(2)}) collective-permute-start(f32[4,1024]{1,0:T(4,128)S(1)} %bitcast.31), channel_id=1, source_target_pairs={{0,16},{16,0},{1,17},{17,1},{2,18},{18,2},{3,19},{19,3},{4,20},{20... | collective-permute-start | bytes 49160 | tf_op jit(solution)/shard_map/ppermute | solution.py:78
  179.9 12.9 %collective-permute-start.2 = (f32[2,4,1024]{2,1,0:T(4,128)S(1)}, f32[2,4,1024]{2,1,0:T(4,128)S(1)}, u32[]{:S(2)}, u32[]{:S(2)}) collective-permute-start(f32[2,4,1024]{2,1,0:T(4,128)S(1)} %pad_maximum_fusion), channel_id=1, source_target_pairs={{0,64},{32,96},{64,0},{96,32},{1,65},{33,97},{65,1},{97,33},{2,66}... | collective-permute-start | bytes 98312 | tf_op jit(solution)/shard_map/ppermute | solution.py:84
  189.6 3.2 %collective-permute-start.1 = (f32[2,4,1024]{2,1,0:T(4,128)S(1)}, f32[2,4,1024]{2,1,0:T(4,128)S(1)}, u32[]{:S(2)}, u32[]{:S(2)}) collective-permute-start(f32[2,4,1024]{2,1,0:T(4,128)S(1)} %pad_maximum_fusion), channel_id=1, source_target_pairs={{0,96},{32,0},{64,32},{96,64},{1,97},{33,1},{65,33},{97,65},{2,98}... | collective-permute-start | bytes 98312 | tf_op jit(solution)/shard_map/ppermute | solution.py:84
  189.6 4.4 %collective-permute-start.3 = (f32[2,4,1024]{2,1,0:T(4,128)S(1)}, f32[2,4,1024]{2,1,0:T(4,128)S(1)}, u32[]{:S(2)}, u32[]{:S(2)}) collective-permute-start(f32[2,4,1024]{2,1,0:T(4,128)S(1)} %pad_maximum_fusion), channel_id=1, source_target_pairs={{0,32},{32,64},{64,96},{96,0},{1,33},{33,65},{65,97},{97,1},{2,34}... | collective-permute-start | bytes 98312 | tf_op jit(solution)/shard_map/ppermute | solution.py:84

commit v2 on v1

--- a/solution.py
+++ b/solution.py
@@ -11,16 +11,16 @@
 ALL = ROW + COL
 
 
-def order_slots(ids_ref, where_ref, source_ref, out_ref, sems):
+def order_slots(ids_ref, where_ref, source_ref, out_ref, data, load_sems, store_sem):
     count = source_ref.shape[0]
-    copies = []
+    loads = [pltpu.make_async_copy(source_ref.at[j], data.at[j], load_sems.at[j]) for j in range(count)]
+    for load in loads:
+        load.start()
     for slot in range(count):
         block = ids_ref[slot, where_ref[0]] // where_ref[1]
-        copy = pltpu.make_async_copy(source_ref.at[slot], out_ref.at[block], sems.at[slot])
-        copy.start()
-        copies.append(copy)
-    for copy in copies:
-        copy.wait()
+        loads[slot].wait()
+        pltpu.make_async_copy(data.at[slot], out_ref.at[block], store_sem).start()
+    pltpu.make_async_copy(data, out_ref, store_sem).wait()
 
 
 def place_and_reduce(place_ref, factor_ref, received_ref, relaid_ref, share_ref, data, sums, load_sems, store_sem):
@@ -63,7 +63,7 @@
             lanes = slice(i * 64, (i + 1) * 64)
             share_ref[c + i, :half, :] = jnp.concatenate([shares[:half, lanes], shares[half:, lanes]], axis=1)
             share_ref[c + i, half:, :] = jnp.concatenate([squares[:, lanes], squares[:, lanes]], axis=1)
-    pltpu.make_async_copy(data, data, store_sem).wait()
+    pltpu.make_async_copy(received_ref, relaid_ref, store_sem).wait()
 
 
 def finish(shares_ref, projection_ref, norms_ref, *, full_width):
@@ -74,8 +74,7 @@
     norms_ref[...] = jnp.sqrt(total[half : half + 1, :64] / full_width + epsilon)
 
 
-def gathered_factor(shard):
-    other = lax.ppermute(shard, "yh", [(0, 1), (1, 0)])
+def gathered_factor(shard, other):
     low = lax.axis_index("yh") == 0
     pair = jnp.stack([jnp.where(low, shard, other), jnp.where(low, other, shard)])
     count = lax.axis_size("x")
@@ -99,20 +98,26 @@
     own_rows = devices * group_rows // columns_total
     ids = group_map.T.astype(jnp.int32)
     source = old_residual.reshape(rows_total, group_rows, columns_total, width).transpose(0, 2, 1, 3)
-    any_space = pl.BlockSpec(memory_space=pl.ANY)
+    hbm = pl.BlockSpec(memory_space=pltpu.HBM)
     smem = pl.BlockSpec(memory_space=pltpu.SMEM)
     vmem = pl.BlockSpec(memory_space=pltpu.VMEM)
+    shard = q_factor.T
+    other = lax.ppermute(shard, "yh", [(0, 1), (1, 0)])
     pieces = pl.pallas_call(
         order_slots,
         out_shape=jax.ShapeDtypeStruct(source.shape, jnp.float32),
-        in_specs=[smem, smem, any_space],
-        out_specs=any_space,
-        scratch_shapes=[pltpu.SemaphoreType.DMA((rows_total,))],
+        in_specs=[smem, smem, hbm],
+        out_specs=hbm,
+        scratch_shapes=[
+            pltpu.VMEM(source.shape, jnp.float32),
+            pltpu.SemaphoreType.DMA((rows_total,)),
+            pltpu.SemaphoreType.DMA,
+        ],
         name="order_slots",
     )(ids, jnp.stack([position, jnp.int32(devices)]), source)
-    pieces = pieces.reshape(devices, group_rows, width)
+    pieces, other = lax.optimization_barrier((pieces.reshape(devices, group_rows, width), other))
     received = lax.all_to_all(pieces, ALL, 0, 0, tiled=True)
-    factor = gathered_factor(q_factor.T)
+    factor = gathered_factor(shard, other)
     place = jnp.sum(jnp.where(ids // devices == my_row, ids % devices, 0), axis=0)
     blocks = 8
     relaid, shares = pl.pallas_call(
@@ -121,8 +126,8 @@
             jax.ShapeDtypeStruct((devices, group_rows, width), jnp.float32),
             jax.ShapeDtypeStruct((columns_total, rank // 2 + 8, 2 * own_rows), jnp.float32),
         ),
-        in_specs=[smem, vmem, any_space],
-        out_specs=(any_space, vmem),
+        in_specs=[smem, vmem, hbm],
+        out_specs=(hbm, vmem),
         scratch_shapes=[
             pltpu.VMEM((blocks, devices // blocks, group_rows, width), jnp.float32),
             pltpu.VMEM((devices * group_rows, 128), jnp.float32),

time: 222 us -> 93.9 us (0.42)
  Pallas kernels: 137 us -> 12.7 us
  waiting for transfers between devices: 37.4 us -> 46.8 us
  starting transfers between devices: 26.1 us -> 17.5 us
  blocking collectives: 18.3 us -> 13.7 us
    pallas_call x1, Pallas kernels: 129 us -> 4.24 us  [on_device(): pl.pallas_call(order_slots, out_shape=jax.ShapeDtypeStruct(source.shape,...]
    ppermute x3, waiting for transfers between devices: 2.87 us -> 44.9 us  [gathered_factor(): lax.ppermute(pair, 'x', [(i, (i - step) % count) for i in range(count)])]
    ppermute x1, waiting for transfers between devices: 34.1 us -> 0.01 us  [on_device(): other = lax.ppermute(shard, 'yh', [(0, 1), (1, 0)])]
    ppermute x3, starting transfers between devices: 11.2 us -> 4.4 us  [gathered_factor(): lax.ppermute(pair, 'x', [(i, (i - step) % count) for i in range(count)])]
    all_to_all x1, blocking collectives: 18.3 us -> 13.7 us  [on_device(): shares = lax.all_to_all(shares, COL, 0, 0, tiled=True)]
    all_to_all x1, starting transfers between devices: 12 us -> 9.27 us  [on_device(): received = lax.all_to_all(pieces, ALL, 0, 0, tiled=True)]
  transfers between devices with their start and end apart: 5 -> 5, of which waited for: 4 -> 3; matrix products, arithmetic and copies ran while one was open for 1% -> 2% of each run, Pallas kernels for 0% -> 5%
where the time goes in v2:
time: 93.9 us; the launch traced here: 93.5 us
  waiting for transfers between devices  46.8 us (50%)
  starting transfers between devices  17.5 us (19%)
  blocking collectives  13.7 us (15%)
  Pallas kernels  12.7 us (14%)
  other arithmetic  1.16 us (1%)
    ppermute x3, waiting for transfers between devices, gathered_factor(): lax.ppermute(pair, 'x', [(i, (i - step) % count) for i in range(count)])  44.9 us
    all_to_all x1, blocking collectives, on_device(): shares = lax.all_to_all(shares, COL, 0, 0, tiled=True)  13.7 us
    all_to_all x1, starting transfers between devices, on_device(): received = lax.all_to_all(pieces, ALL, 0, 0, tiled=True)  9.27 us
    pallas_call x1, Pallas kernels, on_device(): pl.pallas_call(place_and_reduce, out_shape=(jax.ShapeDtypeStruct((devices...  6.84 us
    ppermute x3, starting transfers between devices, gathered_factor(): lax.ppermute(pair, 'x', [(i, (i - step) % count) for i in range(count)])  4.4 us
    pallas_call x1, Pallas kernels, on_device(): pl.pallas_call(order_slots, out_shape=jax.ShapeDtypeStruct(source.shape,...  4.24 us
    ppermute x1, starting transfers between devices, on_device(): other = lax.ppermute(shard, 'yh', [(0, 1), (1, 0)])  3.81 us
    all_to_all x1, waiting for transfers between devices, on_device(): received = lax.all_to_all(pieces, ALL, 0, 0, tiled=True)  1.95 us
  transfers between devices with their start and end apart: 5, of which 3 were waited for; matrix products, arithmetic and copies ran while one was open for 2% of the time, Pallas kernels for 5%

profile of v2, /device:TPU:1, one launch (start us, length us, event | category | flops | bytes accessed | tf_op | source)
XLA Modules:
  0.0 93.5 jit_solution(10314334994799699530)
XLA Ops:
  0.6 3.8 %collective-permute-start = (f32[4,1024]{1,0:T(4,128)}, f32[4,1024]{1,0:T(4,128)S(1)}, u32[]{:S(2)}, u32[]{:S(2)}) collective-permute-start(f32[4,1024]{1,0:T(4,128)} %bitcast.31), channel_id=1, source_target_pairs={{0,16},{16,0},{1,17},{17,1},{2,18},{18,2},{3,19},{19,3},{4,20},{20... | collective-permute-start | bytes 49160 | tf_op jit(solution)/shard_map/ppermute | solution.py:105
  4.4 0.6 pad_add_fusion.where_ref
  5.0 4.2 %order_slots.1 = f32[8,16,8,1024]{3,2,1,0:T(8,128)} custom-call(s32[8,128]{1,0:T(8,128)} %bitcast.30, s32[2]{0:T(128)} %pad_add_fusion.where_ref, f32[8,16,8,1024]{3,2,1,0:T(8,128)} %bitcast.29), custom_call_target="tpu_custom_call" | custom-call | tf_op jit(solution)/shard_map/order_slots/pallas_call | solution.py:106
  9.3 0.0 collective-permute-done
  9.3 0.0 copy-start
  9.3 0.0 copy-start.1
  9.3 9.3 %all-to-all-start = ((f32[128,8,1024]{2,1,0:T(8,128)}), f32[128,8,1024]{2,1,0:T(8,128)}, u32[]{:S(2)}, u32[]{:S(2)}) async-start(f32[128,8,1024]{2,1,0:T(8,128)} %bitcast.28), calls=%async_computation | async-start | bytes 8388608 | tf_op jit(solution)/shard_map/all_to_all | solution.py:119
  18.6 0.0 copy-done
  18.6 0.5 fusion.2.place_ref
  19.2 0.0 copy-done.1
  19.2 2.9 %collective-permute-start.2 = (f32[2,4,1024]{2,1,0:T(4,128)S(1)}, f32[2,4,1024]{2,1,0:T(4,128)S(1)}, u32[]{:S(2)}, u32[]{:S(2)}) collective-permute-start(f32[2,4,1024]{2,1,0:T(4,128)S(1)} %pad_maximum_fusion), channel_id=1, source_target_pairs={{0,64},{32,96},{64,0},{96,32},{1,65},{33,97},{65,1},{97,33},{2,66}... | collective-permute-start | bytes 98312 | tf_op jit(solution)/shard_map/ppermute | solution.py:83
  22.1 0.9 collective-permute-start.1
  23.0 0.6 collective-permute-start.3
  23.6 44.0 %collective-permute-done.1 = f32[2,4,1024]{2,1,0:T(4,128)S(1)} collective-permute-done((f32[2,4,1024]{2,1,0:T(4,128)S(1)}, f32[2,4,1024]{2,1,0:T(4,128)S(1)}, u32[]{:S(2)}, u32[]{:S(2)}) %collective-permute-start.1) | collective-permute-done | bytes 32800 | tf_op jit(solution)/shard_map/ppermute | solution.py:83
  67.7 0.0 collective-permute-done.2
  67.7 0.8 collective-permute-done.3
  68.6 0.7 reshape.23.factor_ref
  69.3 2.0 %all-to-all-done.received_ref = f32[128,8,1024]{2,1,0:T(8,128)} async-done(((f32[128,8,1024]{2,1,0:T(8,128)}), f32[128,8,1024]{2,1,0:T(8,128)}, u32[]{:S(2)}, u32[]{:S(2)}) %all-to-all-start) | async-done | bytes 4194336 | tf_op jit(solution)/shard_map/all_to_all | solution.py:119
  71.3 6.8 %place_and_reduce.1 = (f32[128,8,1024]{2,1,0:T(8,128)}, f32[16,24,128]{2,1,0:T(8,128)}) custom-call(s32[128]{0:T(128)} %fusion.2.place_ref, f32[32,1024]{1,0:T(8,128)} %reshape.23.factor_ref, f32[128,8,1024]{2,1,0:T(8,128)} %all-to-all-done.received_ref), custom_call_target="tpu_custom_call" | custom-call | tf_op jit(solution)/shard_map/place_and_reduce/pallas_call | solution.py:123
  78.1 13.7 %all_to_all.10.refs_0_ = f32[16,24,128]{2,1,0:T(8,128)} all-to-all(f32[16,24,128]{2,1,0:T(8,128)} %get-tuple-element.12), channel_id=1, replica_groups=mesh['x'=4,'yh'=2,'z'=4,'yl'=2,'core'=2] {'z','yl','core'}, dimensions={0} | all-to-all | bytes 393216 | tf_op jit(solution)/shard_map/all_to_all | solution.py:139
  91.9 1.6 %finish.1 = (f32[32,64]{1,0:T(8,128)}, f32[1,64]{1,0:T(1,128)}) custom-call(f32[16,24,128]{2,1,0:T(8,128)} %all_to_all.10.refs_0_), custom_call_target="tpu_custom_call" | custom-call | tf_op jit(solution)/shard_map/finish/pallas_call | solution.py:140
  (11 shorter events, 0.1 us)
Async XLA Ops:
  0.6 8.7 %collective-permute-start = (f32[4,1024]{1,0:T(4,128)}, f32[4,1024]{1,0:T(4,128)S(1)}, u32[]{:S(2)}, u32[]{:S(2)}) collective-permute-start(f32[4,1024]{1,0:T(4,128)} %bitcast.31), channel_id=1, source_target_pairs={{0,16},{16,0},{1,17},{17,1},{2,18},{18,2},{3,19},{19,3},{4,20},{20... | collective-permute-start | bytes 49160 | tf_op jit(solution)/shard_map/ppermute | solution.py:105
  9.3 9.3 %copy-start = (s32[128,8]{0,1:T(8,128)S(1)}, s32[128,8]{0,1:T(8,128)}, u32[]{:S(2)}) copy-start(s32[128,8]{0,1:T(8,128)} %param.4) | copy-start | bytes 12292
  9.3 9.9 %copy-start.1 = (f32[1024,4]{0,1:T(4,128)S(1)}, f32[1024,4]{0,1:T(4,128)}, u32[]{:S(2)}) copy-start(f32[1024,4]{0,1:T(4,128)} %param.5) | copy-start | bytes 49156
  9.3 62.0 %all-to-all-start = ((f32[128,8,1024]{2,1,0:T(8,128)}), f32[128,8,1024]{2,1,0:T(8,128)}, u32[]{:S(2)}, u32[]{:S(2)}) async-start(f32[128,8,1024]{2,1,0:T(8,128)} %bitcast.28), calls=%async_computation | async-start | bytes 8388608 | tf_op jit(solution)/shard_map/all_to_all | solution.py:119
  19.2 48.5 %collective-permute-start.2 = (f32[2,4,1024]{2,1,0:T(4,128)S(1)}, f32[2,4,1024]{2,1,0:T(4,128)S(1)}, u32[]{:S(2)}, u32[]{:S(2)}) collective-permute-start(f32[2,4,1024]{2,1,0:T(4,128)S(1)} %pad_maximum_fusion), channel_id=1, source_target_pairs={{0,64},{32,96},{64,0},{96,32},{1,65},{33,97},{65,1},{97,33},{2,66}... | collective-permute-start | bytes 98312 | tf_op jit(solution)/shard_map/ppermute | solution.py:83
  22.1 45.5 %collective-permute-start.1 = (f32[2,4,1024]{2,1,0:T(4,128)S(1)}, f32[2,4,1024]{2,1,0:T(4,128)S(1)}, u32[]{:S(2)}, u32[]{:S(2)}) collective-permute-start(f32[2,4,1024]{2,1,0:T(4,128)S(1)} %pad_maximum_fusion), channel_id=1, source_target_pairs={{0,96},{32,0},{64,32},{96,64},{1,97},{33,1},{65,33},{97,65},{2,98}... | collective-permute-start | bytes 98312 | tf_op jit(solution)/shard_map/ppermute | solution.py:83
  23.0 45.5 %collective-permute-start.3 = (f32[2,4,1024]{2,1,0:T(4,128)S(1)}, f32[2,4,1024]{2,1,0:T(4,128)S(1)}, u32[]{:S(2)}, u32[]{:S(2)}) collective-permute-start(f32[2,4,1024]{2,1,0:T(4,128)S(1)} %pad_maximum_fusion), channel_id=1, source_target_pairs={{0,32},{32,64},{64,96},{96,0},{1,33},{33,65},{65,97},{97,1},{2,34}... | collective-permute-start | bytes 98312 | tf_op jit(solution)/shard_map/ppermute | solution.py:83
